TPU v7x, 256 devices: a whole 4x4x8 slice. The times are simulated.
256 devices in a mesh: seq: 32 (over z, x_hi, core), head: 4 (over y), batch: 2 (over x_lo).
Axes of the slice: x: 4 (x_hi: 2, x_lo: 2; x = x_hi * 2 + x_lo), y: 4, z: 8, core: 2. Of those that a mesh axis runs over, the one named last changes fastest.
Arguments:
- queries: bfloat16 [16384, 4096], P(('batch', 'seq', 'head')), parts along dimension 0, may hold values from -6 to 6
- keys: bfloat16 [16384, 512], P(('batch', 'seq', 'head')), parts along dimension 0, may hold values from -6 to 6
- values: bfloat16 [16384, 512], P(('batch', 'seq', 'head')), parts along dimension 0, may hold values from -6 to 6
- page_of_block: int32 [32], P('batch'), parts along dimension 0, may hold values from 0 to 8, never falling along the last dimension, each value on 1 to 4 neighbouring positions
- links: int32 [32, 16], P('batch'), parts along dimension 0, may hold values 0 or 1
Outputs:
- attended: bfloat16 [16384, 4096], P(('batch', 'seq', 'head')), parts along dimension 0
There are 2 independent parts, one for each index of `batch`. A program takes and returns all parts, laid end to end along the dimension named above; each array names one. Nothing has to cross between parts.
Inputs may be any that keep to these rules, and one draw needn't show every extreme that they name: `page_of_block`: page numbers never fall from one block to the next.
All inputs are finite; a program needn't handle non-finite values.
Results may differ from a plain program's by a relative error of at most 0.0065.
Values may be sent and summed in bfloat16 or wider, within the bound.
A program may use at most 64 MiB of HBM per device.

v0:
```python
import jax
import jax.numpy as jnp
from jax import lax
from jax.sharding import PartitionSpec as P

HEAD_SIZE = 128
BLK = 512


def side_by_side(arrays, axis, dim, along):
    widths = [a.shape[along] for a in arrays]
    both = jnp.concatenate(arrays, axis=along)
    out = lax.all_gather(both, axis, axis=dim, tiled=True)
    return tuple(jnp.split(out, [sum(widths[:k]) for k in range(1, len(widths))], axis=along))


def local(queries, keys, values, page_of_block, links):
    query_all, key_local, value_local = (
        lax.all_to_all(queries, "head", split_axis=1, concat_axis=0, tiled=True),
        lax.all_to_all(keys, "head", split_axis=1, concat_axis=0, tiled=True),
        lax.all_to_all(values, "head", split_axis=1, concat_axis=0, tiled=True),
    )
    row_count = query_all.shape[0]
    kv_here = key_local.shape[1] // HEAD_SIZE
    group_width = query_all.shape[1] // HEAD_SIZE // kv_here
    first_row = lax.axis_index("seq") * row_count
    block_count = page_of_block.shape[0]
    block_ids = jnp.arange(block_count, dtype=jnp.int32)
    page_table = page_of_block.astype(jnp.float32)
    link_table = links.astype(jnp.float32)
    query_pos = first_row + jnp.arange(row_count, dtype=jnp.int32)
    query_onehot = (query_pos[:, None] // BLK == block_ids[None, :]).astype(jnp.float32)
    query_page = jnp.dot(query_onehot, page_table)
    query_links = jnp.dot(query_onehot, link_table)
    query_heads = query_all.reshape(row_count, kv_here, group_width, HEAD_SIZE)
    score_scale = HEAD_SIZE ** (-0.5)

    def block_step(running, key_block, value_block, offset):
        block_rows = key_block.shape[0]
        key_pos = offset + jnp.arange(block_rows, dtype=jnp.int32)
        key_onehot = (key_pos[:, None] // BLK == block_ids[None, :]).astype(jnp.float32)
        key_page = jnp.dot(key_onehot, page_table)
        linked = jnp.dot(query_links, key_onehot.T) > 0.5
        same_page = query_page[:, None] == key_page[None, :]
        allowed = jnp.where(same_page, key_pos[None, :] <= query_pos[:, None], linked)

        def attend(previous):
            maxima, totals, weighted = previous
            scores = (
                jnp.einsum(
                    "rkgd,pkd->kgrp",
                    query_heads,
                    key_block.reshape(block_rows, kv_here, HEAD_SIZE),
                    preferred_element_type=jnp.float32,
                )
                * score_scale
            )
            scores = jnp.where(allowed[None, None], scores, -1e30)
            new_max = jnp.maximum(maxima, jnp.max(scores, axis=-1))
            weights = jnp.where(allowed[None, None], jnp.exp(scores - new_max[..., None]), 0.0)
            factor = jnp.exp(maxima - new_max)
            totals = totals * factor + jnp.sum(weights, axis=-1)
            rounded = weights.astype(jnp.bfloat16)
            weighted = weighted * factor[..., None] + jnp.einsum(
                "kgrp,pkd->kgrd",
                rounded,
                value_block.reshape(block_rows, kv_here, HEAD_SIZE),
                preferred_element_type=jnp.float32,
            )
            return (new_max, totals, weighted)

        return lax.cond(jnp.any(allowed), attend, lambda previous: previous, running)

    initial = (
        jnp.full((kv_here, group_width, row_count), -1e30, jnp.float32),
        jnp.zeros((kv_here, group_width, row_count), jnp.float32),
        jnp.zeros((kv_here, group_width, row_count, HEAD_SIZE), jnp.float32),
    )
    running = initial
    key_piece, value_piece = side_by_side((key_local, value_local), "seq", 0, 1)
    piece_rows = key_piece.shape[0]
    sub_count = piece_rows // BLK
    key_split = key_piece.reshape(sub_count, BLK, key_piece.shape[1])
    value_split = value_piece.reshape(sub_count, BLK, value_piece.shape[1])

    def scan_step(state_now, scan_item):
        key_block, value_block, block_index = scan_item
        return (block_step(state_now, key_block, value_block, block_index * BLK), None)

    running, unused = lax.scan(
        scan_step, running, (key_split, value_split, jnp.arange(sub_count, dtype=jnp.int32))
    )
    maxima, totals, weighted = running
    outcome = weighted / totals[..., None]
    outcome = (
        outcome.transpose(2, 0, 1, 3)
        .reshape(row_count, kv_here * group_width * HEAD_SIZE)
        .astype(jnp.bfloat16)
    )
    return lax.all_to_all(outcome, "head", split_axis=0, concat_axis=1, tiled=True)


def solution(mesh):
    in_specs = (
        P(("batch", "seq", "head"), None),
        P(("batch", "seq", "head"), None),
        P(("batch", "seq", "head"), None),
        P("batch"),
        P("batch", None),
    )
    out_specs = P(("batch", "seq", "head"), None)
    return jax.shard_map(local, mesh=mesh, in_specs=in_specs, out_specs=out_specs, check_vma=False)
```

profile of v0, /device:TPU:96, one launch (start us, length us, event | category | flops | bytes accessed | tf_op | source)
XLA Modules:
  0.0 233.1 jit_solution(11459004962486201272)
XLA Ops:
  6.5 0.8 copy-done
  8.0 4.5 %all-to-all-start = ((bf16[64,4,128]{2,0,1:T(8,128)(2,1)}), bf16[64,4,128]{2,0,1:T(8,128)(2,1)S(1)}, u32[]{:S(2)}, u32[]{:S(2)}) async-start(bf16[64,4,128]{2,0,1:T(8,128)(2,1)} %copy_bitcast_fusion.2), calls=%async_computation | async-start | bytes 131072 | tf_op jit(solution)/shard_map/all_to_all | solution.py:20
  12.5 0.9 copy_bitcast_fusion.1
  13.3 4.8 %all-to-all-done = bf16[64,4,128]{2,0,1:T(8,128)(2,1)S(1)} async-done(((bf16[64,4,128]{2,0,1:T(8,128)(2,1)}), bf16[64,4,128]{2,0,1:T(8,128)(2,1)S(1)}, u32[]{:S(2)}, u32[]{:S(2)}) %all-to-all-start) | async-done | bytes 65568 | tf_op jit(solution)/shard_map/all_to_all | solution.py:20
  18.1 8.0 %all_to_all.70 = bf16[64,4,128]{2,0,1:T(8,128)(2,1)S(1)} all-to-all(bf16[64,4,128]{2,0,1:T(8,128)(2,1)S(1)} %copy_bitcast_fusion.1), channel_id=1, replica_groups=mesh['seq'=32,'head'=4,'batch'=2] {'head'}, dimensions={1} | all-to-all | bytes 131072 | tf_op jit(solution)/shard_map/all_to_all | solution.py:21
  26.1 0.7 pad_maximum_fusion
  26.8 1.9 copy.43
  28.6 3.5 %all-to-all-start.2 = ((bf16[64,4,1024]{2,0,1:T(8,128)(2,1)}), bf16[64,4,1024]{2,0,1:T(8,128)(2,1)S(1)}, u32[]{:S(2)}, u32[]{:S(2)}) async-start(bf16[64,4,1024]{2,0,1:T(8,128)(2,1)} %bitcast.104), calls=%async_computation.2 | async-start | bytes 1048576 | tf_op jit(solution)/shard_map/all_to_all | solution.py:19
  32.8 0.9 fusion.42
  33.7 0.9 fusion.41
  34.6 5.6 %all-to-all-done.2 = bf16[64,4,1024]{2,0,1:T(8,128)(2,1)S(1)} async-done(((bf16[64,4,1024]{2,0,1:T(8,128)(2,1)}), bf16[64,4,1024]{2,0,1:T(8,128)(2,1)S(1)}, u32[]{:S(2)}, u32[]{:S(2)}) %all-to-all-start.2) | async-done | bytes 524320 | tf_op jit(solution)/shard_map/all_to_all | solution.py:19
  40.4 72.5 %all-gather.2.cloned.1.call-done = bf16[8192,256]{1,0:T(8,128)(2,1)} async-done(((bf16[256,256]{1,0:T(8,128)(2,1)}), bf16[8192,256]{1,0:T(8,128)(2,1)}) %all-gather.2.cloned.1.call-update) | async-done | bytes 4194320 | tf_op jit(solution)/shard_map/all_gather | solution.py:13
  112.9 4.5 %fusion.49 = (bf16[8192,128]{1,0:T(8,128)(2,1)}, bf16[8192,128]{1,0:T(8,128)(2,1)}) fusion(bf16[8192,256]{1,0:T(8,128)(2,1)} %all-gather.2.cloned.1.call-done), kind=kLoop, calls=%fused_computation.66 | loop fusion | bytes 8388608 | tf_op jit(solution)/shard_map/split | solution.py:14
  117.4 93.0 %while.19 = (s32[]{:T(128)}, f32[1,8,256]{2,1,0:T(8,128)S(1)}, f32[1,8,256]{2,1,0:T(8,128)S(1)}, f32[1,8,256,128]{3,2,1,0:T(8,128)S(1)}, f32[256]{0:T(256)S(1)},...) while((s32[]{:T(128)}, f32[1,8,256]{2,1,0:T(8,128)S(1)}, ...), condition=%wide.region_6.7_spmd.clone.clone, body=%wide.region_0.6_spmd.clone.clone.sunk | while | flops 555923712 | bytes 16148931 | solution.py:90
  119.0 1.0 fusion.62
  122.1 1.0 fusion.62
  125.3 1.0 fusion.62
  128.5 1.0 fusion.62
  131.7 1.0 fusion.62
  134.8 1.0 fusion.62
  138.0 1.0 fusion.62
  139.6 5.3 %conditional.4 = ((f32[1,8,256]{2,1,0:T(8,128)S(1)}, f32[1,8,256]{2,1,0:T(8,128)S(1)}, f32[1,8,256,128]{3,2,1,0:T(8,128)S(1)})) conditional(s32[]{:T(128)} %convert_element_type.56, (f32[1,8,256]{2,1,0:T(8,128)S(1)}, f32[1,8,256]{2,1,0:T(8,128)S(1)}, f32[1,8,256,128]{3,2,1,0:T(8,128)S(1)}) %tuple.67, (pred[256,512]{0,1:T(8,128)(4,1)S(1)}, ...), branch_computations={%region_2.2_spmd, %region_3.5_spmd} | conditional | flops 551032832 | bytes 15991840 | solution.py:72
  139.7 1.7 fusion.2
  141.4 2.5 %fusion.12 = f32[1,8,256,128]{3,2,1,0:T(8,128)S(1)} fusion(f32[512,256,8]{1,0,2:T(8,128)S(1)} %get-tuple-element.409, f32[8,256]{1,0:T(8,128)S(1)} %bitcast.114, pred[256,512]{0,1:T(8,128)(4,1)S(1)} %get-tuple-element.245, f32[1,8,256,128]{3,2,1,0:T(8,128)S(1)} %get-tuple-element.250, f32[8,256]{1,0:T(8,128)S(1)} %get-tuple-element.406, ...), kind=kOutput, calls=%fused_computation.10 | convolution fusion | flops 274202624 | bytes 6570496 | tf_op jit(solution)/shard_map/while/body/eval_jaxpr/cond/branch_1_fun/kgrp,pkd->kgrd/dot_general | solution.py:64
  143.9 1.0 fusion.4
  146.5 1.0 fusion.62
  149.6 1.0 fusion.62
  151.3 5.3 %conditional.4 = ((f32[1,8,256]{2,1,0:T(8,128)S(1)}, f32[1,8,256]{2,1,0:T(8,128)S(1)}, f32[1,8,256,128]{3,2,1,0:T(8,128)S(1)})) conditional(s32[]{:T(128)} %convert_element_type.56, (f32[1,8,256]{2,1,0:T(8,128)S(1)}, f32[1,8,256]{2,1,0:T(8,128)S(1)}, f32[1,8,256,128]{3,2,1,0:T(8,128)S(1)}) %tuple.67, (pred[256,512]{0,1:T(8,128)(4,1)S(1)}, ...), branch_computations={%region_2.2_spmd, %region_3.5_spmd} | conditional | flops 551032832 | bytes 15991840 | solution.py:72
  151.3 1.7 fusion.2
  153.0 2.5 %fusion.12 = f32[1,8,256,128]{3,2,1,0:T(8,128)S(1)} fusion(f32[512,256,8]{1,0,2:T(8,128)S(1)} %get-tuple-element.409, f32[8,256]{1,0:T(8,128)S(1)} %bitcast.114, pred[256,512]{0,1:T(8,128)(4,1)S(1)} %get-tuple-element.245, f32[1,8,256,128]{3,2,1,0:T(8,128)S(1)} %get-tuple-element.250, f32[8,256]{1,0:T(8,128)S(1)} %get-tuple-element.406, ...), kind=kOutput, calls=%fused_computation.10 | convolution fusion | flops 274202624 | bytes 6570496 | tf_op jit(solution)/shard_map/while/body/eval_jaxpr/cond/branch_1_fun/kgrp,pkd->kgrd/dot_general | solution.py:64
  155.5 1.0 fusion.4
  158.1 1.0 fusion.62
  159.7 5.3 %conditional.4 = ((f32[1,8,256]{2,1,0:T(8,128)S(1)}, f32[1,8,256]{2,1,0:T(8,128)S(1)}, f32[1,8,256,128]{3,2,1,0:T(8,128)S(1)})) conditional(s32[]{:T(128)} %convert_element_type.56, (f32[1,8,256]{2,1,0:T(8,128)S(1)}, f32[1,8,256]{2,1,0:T(8,128)S(1)}, f32[1,8,256,128]{3,2,1,0:T(8,128)S(1)}) %tuple.67, (pred[256,512]{0,1:T(8,128)(4,1)S(1)}, ...), branch_computations={%region_2.2_spmd, %region_3.5_spmd} | conditional | flops 551032832 | bytes 15991840 | solution.py:72
  159.7 1.7 fusion.2
  161.4 2.5 %fusion.12 = f32[1,8,256,128]{3,2,1,0:T(8,128)S(1)} fusion(f32[512,256,8]{1,0,2:T(8,128)S(1)} %get-tuple-element.409, f32[8,256]{1,0:T(8,128)S(1)} %bitcast.114, pred[256,512]{0,1:T(8,128)(4,1)S(1)} %get-tuple-element.245, f32[1,8,256,128]{3,2,1,0:T(8,128)S(1)} %get-tuple-element.250, f32[8,256]{1,0:T(8,128)S(1)} %get-tuple-element.406, ...), kind=kOutput, calls=%fused_computation.10 | convolution fusion | flops 274202624 | bytes 6570496 | tf_op jit(solution)/shard_map/while/body/eval_jaxpr/cond/branch_1_fun/kgrp,pkd->kgrd/dot_general | solution.py:64
  164.0 1.0 fusion.4
  166.6 1.0 fusion.62
  168.2 5.3 %conditional.4 = ((f32[1,8,256]{2,1,0:T(8,128)S(1)}, f32[1,8,256]{2,1,0:T(8,128)S(1)}, f32[1,8,256,128]{3,2,1,0:T(8,128)S(1)})) conditional(s32[]{:T(128)} %convert_element_type.56, (f32[1,8,256]{2,1,0:T(8,128)S(1)}, f32[1,8,256]{2,1,0:T(8,128)S(1)}, f32[1,8,256,128]{3,2,1,0:T(8,128)S(1)}) %tuple.67, (pred[256,512]{0,1:T(8,128)(4,1)S(1)}, ...), branch_computations={%region_2.2_spmd, %region_3.5_spmd} | conditional | flops 551032832 | bytes 15991840 | solution.py:72
  168.2 1.7 fusion.2
  169.9 2.5 %fusion.12 = f32[1,8,256,128]{3,2,1,0:T(8,128)S(1)} fusion(f32[512,256,8]{1,0,2:T(8,128)S(1)} %get-tuple-element.409, f32[8,256]{1,0:T(8,128)S(1)} %bitcast.114, pred[256,512]{0,1:T(8,128)(4,1)S(1)} %get-tuple-element.245, f32[1,8,256,128]{3,2,1,0:T(8,128)S(1)} %get-tuple-element.250, f32[8,256]{1,0:T(8,128)S(1)} %get-tuple-element.406, ...), kind=kOutput, calls=%fused_computation.10 | convolution fusion | flops 274202624 | bytes 6570496 | tf_op jit(solution)/shard_map/while/body/eval_jaxpr/cond/branch_1_fun/kgrp,pkd->kgrd/dot_general | solution.py:64
  172.4 1.0 fusion.4
  175.0 1.0 fusion.62
  176.6 5.3 %conditional.4 = ((f32[1,8,256]{2,1,0:T(8,128)S(1)}, f32[1,8,256]{2,1,0:T(8,128)S(1)}, f32[1,8,256,128]{3,2,1,0:T(8,128)S(1)})) conditional(s32[]{:T(128)} %convert_element_type.56, (f32[1,8,256]{2,1,0:T(8,128)S(1)}, f32[1,8,256]{2,1,0:T(8,128)S(1)}, f32[1,8,256,128]{3,2,1,0:T(8,128)S(1)}) %tuple.67, (pred[256,512]{0,1:T(8,128)(4,1)S(1)}, ...), branch_computations={%region_2.2_spmd, %region_3.5_spmd} | conditional | flops 551032832 | bytes 15991840 | solution.py:72
  176.6 1.7 fusion.2
  178.4 2.5 %fusion.12 = f32[1,8,256,128]{3,2,1,0:T(8,128)S(1)} fusion(f32[512,256,8]{1,0,2:T(8,128)S(1)} %get-tuple-element.409, f32[8,256]{1,0:T(8,128)S(1)} %bitcast.114, pred[256,512]{0,1:T(8,128)(4,1)S(1)} %get-tuple-element.245, f32[1,8,256,128]{3,2,1,0:T(8,128)S(1)} %get-tuple-element.250, f32[8,256]{1,0:T(8,128)S(1)} %get-tuple-element.406, ...), kind=kOutput, calls=%fused_computation.10 | convolution fusion | flops 274202624 | bytes 6570496 | tf_op jit(solution)/shard_map/while/body/eval_jaxpr/cond/branch_1_fun/kgrp,pkd->kgrd/dot_general | solution.py:64
  180.9 1.0 fusion.4
  183.5 1.0 fusion.62
  186.6 1.0 fusion.62
  188.3 5.3 %conditional.4 = ((f32[1,8,256]{2,1,0:T(8,128)S(1)}, f32[1,8,256]{2,1,0:T(8,128)S(1)}, f32[1,8,256,128]{3,2,1,0:T(8,128)S(1)})) conditional(s32[]{:T(128)} %convert_element_type.56, (f32[1,8,256]{2,1,0:T(8,128)S(1)}, f32[1,8,256]{2,1,0:T(8,128)S(1)}, f32[1,8,256,128]{3,2,1,0:T(8,128)S(1)}) %tuple.67, (pred[256,512]{0,1:T(8,128)(4,1)S(1)}, ...), branch_computations={%region_2.2_spmd, %region_3.5_spmd} | conditional | flops 551032832 | bytes 15991840 | solution.py:72
  188.3 1.7 fusion.2
  190.0 2.5 %fusion.12 = f32[1,8,256,128]{3,2,1,0:T(8,128)S(1)} fusion(f32[512,256,8]{1,0,2:T(8,128)S(1)} %get-tuple-element.409, f32[8,256]{1,0:T(8,128)S(1)} %bitcast.114, pred[256,512]{0,1:T(8,128)(4,1)S(1)} %get-tuple-element.245, f32[1,8,256,128]{3,2,1,0:T(8,128)S(1)} %get-tuple-element.250, f32[8,256]{1,0:T(8,128)S(1)} %get-tuple-element.406, ...), kind=kOutput, calls=%fused_computation.10 | convolution fusion | flops 274202624 | bytes 6570496 | tf_op jit(solution)/shard_map/while/body/eval_jaxpr/cond/branch_1_fun/kgrp,pkd->kgrd/dot_general | solution.py:64
  192.5 1.0 fusion.4
  195.1 1.0 fusion.62
  196.7 5.3 %conditional.4 = ((f32[1,8,256]{2,1,0:T(8,128)S(1)}, f32[1,8,256]{2,1,0:T(8,128)S(1)}, f32[1,8,256,128]{3,2,1,0:T(8,128)S(1)})) conditional(s32[]{:T(128)} %convert_element_type.56, (f32[1,8,256]{2,1,0:T(8,128)S(1)}, f32[1,8,256]{2,1,0:T(8,128)S(1)}, f32[1,8,256,128]{3,2,1,0:T(8,128)S(1)}) %tuple.67, (pred[256,512]{0,1:T(8,128)(4,1)S(1)}, ...), branch_computations={%region_2.2_spmd, %region_3.5_spmd} | conditional | flops 551032832 | bytes 15991840 | solution.py:72
  196.7 1.7 fusion.2
  198.4 2.5 %fusion.12 = f32[1,8,256,128]{3,2,1,0:T(8,128)S(1)} fusion(f32[512,256,8]{1,0,2:T(8,128)S(1)} %get-tuple-element.409, f32[8,256]{1,0:T(8,128)S(1)} %bitcast.114, pred[256,512]{0,1:T(8,128)(4,1)S(1)} %get-tuple-element.245, f32[1,8,256,128]{3,2,1,0:T(8,128)S(1)} %get-tuple-element.250, f32[8,256]{1,0:T(8,128)S(1)} %get-tuple-element.406, ...), kind=kOutput, calls=%fused_computation.10 | convolution fusion | flops 274202624 | bytes 6570496 | tf_op jit(solution)/shard_map/while/body/eval_jaxpr/cond/branch_1_fun/kgrp,pkd->kgrd/dot_general | solution.py:64
  201.0 1.0 fusion.4
  203.5 1.0 fusion.62
  205.2 5.3 %conditional.4 = ((f32[1,8,256]{2,1,0:T(8,128)S(1)}, f32[1,8,256]{2,1,0:T(8,128)S(1)}, f32[1,8,256,128]{3,2,1,0:T(8,128)S(1)})) conditional(s32[]{:T(128)} %convert_element_type.56, (f32[1,8,256]{2,1,0:T(8,128)S(1)}, f32[1,8,256]{2,1,0:T(8,128)S(1)}, f32[1,8,256,128]{3,2,1,0:T(8,128)S(1)}) %tuple.67, (pred[256,512]{0,1:T(8,128)(4,1)S(1)}, ...), branch_computations={%region_2.2_spmd, %region_3.5_spmd} | conditional | flops 551032832 | bytes 15991840 | solution.py:72
  205.2 1.7 fusion.2
  206.9 2.5 %fusion.12 = f32[1,8,256,128]{3,2,1,0:T(8,128)S(1)} fusion(f32[512,256,8]{1,0,2:T(8,128)S(1)} %get-tuple-element.409, f32[8,256]{1,0:T(8,128)S(1)} %bitcast.114, pred[256,512]{0,1:T(8,128)(4,1)S(1)} %get-tuple-element.245, f32[1,8,256,128]{3,2,1,0:T(8,128)S(1)} %get-tuple-element.250, f32[8,256]{1,0:T(8,128)S(1)} %get-tuple-element.406, ...), kind=kOutput, calls=%fused_computation.10 | convolution fusion | flops 274202624 | bytes 6570496 | tf_op jit(solution)/shard_map/while/body/eval_jaxpr/cond/branch_1_fun/kgrp,pkd->kgrd/dot_general | solution.py:64
  209.4 1.0 fusion.4
  211.4 14.0 %all_to_all.71 = bf16[4,64,1024]{2,1,0:T(8,128)(2,1)S(1)} all-to-all(bf16[4,64,1024]{2,1,0:T(8,128)(2,1)S(1)} %convert_element_type.35), channel_id=1, replica_groups=mesh['seq'=32,'head'=4,'batch'=2] {'head'}, dimensions={0} | all-to-all | bytes 1048576 | tf_op jit(solution)/shard_map/all_to_all | solution.py:100
  225.4 0.8 copy.38
  (111 shorter events, 16.4 us)
Async XLA Ops:
  6.5 0.8 copy-start
  8.0 10.1 %all-to-all-start = ((bf16[64,4,128]{2,0,1:T(8,128)(2,1)}), bf16[64,4,128]{2,0,1:T(8,128)(2,1)S(1)}, u32[]{:S(2)}, u32[]{:S(2)}) async-start(bf16[64,4,128]{2,0,1:T(8,128)(2,1)} %copy_bitcast_fusion.2), calls=%async_computation | async-start | bytes 131072 | tf_op jit(solution)/shard_map/all_to_all | solution.py:20
  12.5 100.4 %all-gather.2.cloned.1.call-start = ((), (), s32[]{:S(2)}) async-start(), calls=%async_computation.4 | async-start | bytes 4325376 | tf_op jit(solution)/shard_map/all_gather | solution.py:13
  28.6 11.5 %all-to-all-start.2 = ((bf16[64,4,1024]{2,0,1:T(8,128)(2,1)}), bf16[64,4,1024]{2,0,1:T(8,128)(2,1)S(1)}, u32[]{:S(2)}, u32[]{:S(2)}) async-start(bf16[64,4,1024]{2,0,1:T(8,128)(2,1)} %bitcast.104), calls=%async_computation.2 | async-start | bytes 1048576 | tf_op jit(solution)/shard_map/all_to_all | solution.py:19
Sparse Core Ops, SparseCore 0:
  26.9 85.9 all-gather.1
where the time goes:
time: 236 us; the launch traced here: 233 us
  waiting for transfers between devices  82.9 us (35%)
  matrix products  55 us (23%)
  blocking collectives  21.9 us (9%)
  loops' own time  21.9 us (9%)
  local copies, waits for them, and re-layouts  19.8 us (8%)
  between operations  13.5 us (6%)
  other arithmetic  10.1 us (4%)
  starting transfers between devices  7.94 us (3%)
    all_gather x1, waiting for transfers between devices, side_by_side(): out = lax.all_gather(both, axis, axis=dim, tiled=True)  72.5 us
    another operation x1, loops' own time, local(): lax.scan(scan_step, running, (key_split, value_split, jnp.arange(sub_coun...  21.4 us
    dot_general x8, matrix products, attend(): jnp.einsum('kgrp,pkd->kgrd', rounded, value_block.reshape(block_rows, kv_...  20.2 us
    dot_general x16, matrix products, block_step(): linked = jnp.dot(query_links, key_onehot.T) > 0.5  15.6 us
    all_to_all x1, blocking collectives, local(): lax.all_to_all(outcome, 'head', split_axis=0, concat_axis=1, tiled=True)  14 us
    dot_general x8, matrix products, attend(): jnp.einsum('rkgd,pkd->kgrp', query_heads, key_block.reshape(block_rows, k...  13.5 us
    dynamic_slice x16, local copies, waits for them, and re-layouts, local(): lax.scan(scan_step, running, (key_split, value_split, jnp.arange(sub_coun...  9.42 us
    reduce_sum x8, other arithmetic, attend(): totals = totals * factor + jnp.sum(weights, axis=-1)  8.08 us
  transfers between devices with their start and end apart: 3, of which 3 were waited for; matrix products, arithmetic and copies ran while one was open for 2% of the time, Pallas kernels for 0%

commit v1 on v0

v1 whole, which is shorter than its diff:
```python
import jax
import jax.numpy as jnp
from jax import lax
from jax.experimental import pallas as pl
from jax.experimental.pallas import tpu as pltpu
from jax.sharding import PartitionSpec as P

HEAD_SIZE = 128
BLK = 512
BLOCKS = 16
HEADS = 8
SEQ = 32
TOKENS = 64
ROWS = 256
WIDE = HEADS * HEAD_SIZE
UNIT = 2
UNITS = HEADS // UNIT
M = UNIT * ROWS
SCALE = HEAD_SIZE ** (-0.5) * 1.4426950408889634
NEG = -1e30
NT = (((1,), (1,)), ((), ()))
F32, BF16 = jnp.float32, jnp.bfloat16


def kernel(
    page_ref, link_ref, q_ref, k_ref, v_ref, out_ref,
    kv, qb, ost, m_s, acc_s, s_s, sh_s, al_s,
    a2a_send, a2a_recv, q_send, q_recv, ring_send, ring_recv, sib_send, sib_recv, out_send, out_recv, loc,
):
    seq, head = lax.axis_index("seq"), lax.axis_index("head")
    z, xh, core = seq // 4, (seq // 2) % 2, seq % 2
    own = seq // 2
    sibling = seq + 1 - 2 * core
    partner = seq + 2 - 4 * xh
    up, down = (seq + 4) % SEQ, (seq + SEQ - 4) % SEQ
    peers = [(head + d) % 4 for d in range(4)]
    half = pl.ds(pl.multiple_of(core * ROWS, ROWS), ROWS)

    def remote(src, dst, send, recv, **where):
        return pltpu.make_async_remote_copy(
            src_ref=src, dst_ref=dst, send_sem=send, recv_sem=recv,
            device_id=where, device_id_type=pl.DeviceIdType.MESH,
        )

    def kv_piece(xo, d, kind):
        src = (k_ref, v_ref)[kind].at[:, pl.ds(pl.multiple_of(peers[d] * HEAD_SIZE, HEAD_SIZE), HEAD_SIZE)]
        dst = kv.at[own, kind, pl.ds(pl.multiple_of(core * ROWS + head * TOKENS, TOKENS), TOKENS), :]
        if xo == 0 and d == 0:
            return pltpu.make_async_copy(src, dst, loc.at[kind])
        where = {"head": peers[d]} if xo == 0 else {"seq": partner, "head": peers[d]}
        return remote(src, dst, a2a_send.at[xo, d, kind], a2a_recv.at[xo, d, kind], **where)

    def q_piece(d, part):
        src = q_ref.at[:, pl.ds(pl.multiple_of(peers[d] * WIDE + part * (WIDE // 2), WIDE // 2), WIDE // 2)]
        dst = qb.at[pl.ds(pl.multiple_of(head * TOKENS, TOKENS), TOKENS), pl.ds(part * (WIDE // 2), WIDE // 2)]
        if d == 0:
            return pltpu.make_async_copy(src, dst, loc.at[2 + part])
        return remote(src, dst, q_send.at[d, part], q_recv.at[d, part], head=peers[d])

    def ring(block, way, step, kind):
        ref = kv.at[block, kind, half, :]
        to = up + way * (down - up)
        return remote(ref, ref, ring_send.at[way, step, kind], ring_recv.at[way, step, kind], seq=to)

    def share(pos, block, kind):
        ref = kv.at[block, kind, half, :]
        return remote(ref, ref, sib_send.at[pos, kind], sib_recv.at[pos, kind], seq=sibling)

    def out_piece(u, d):
        cols = UNIT * HEAD_SIZE
        src = ost.at[pl.ds(pl.multiple_of(peers[d] * TOKENS, TOKENS), TOKENS), pl.ds(u * cols, cols)]
        dst = out_ref.at[:, pl.ds(pl.multiple_of(head * WIDE + u * cols, cols), cols)]
        if d == 0:
            return pltpu.make_async_copy(src, dst, loc.at[4 + u])
        return remote(src, dst, out_send.at[u, d], out_recv.at[u, d], head=peers[d])

    def block_at(pos):
        pair, way = pos // 2, pos % 2
        far = (pair + 1) // 2
        other = (pair + 1) % 2 + pos // 15
        zz = (z + 8 - far + way * 2 * far) % 8
        return zz * 2 + xh + other - 2 * xh * other

    def bias_of(block):
        same = page_ref[own] == page_ref[block]
        allowed = jnp.where(same, (block < own).astype(jnp.int32), link_ref[own, block])
        return jnp.where(allowed == 1, 0.0, NEG).astype(F32)

    barrier = pltpu.get_barrier_semaphore()
    for d in range(1, 4):
        pl.semaphore_signal(barrier, inc=1, device_id={"head": peers[d]}, device_id_type=pl.DeviceIdType.MESH)
    for d in range(4):
        pl.semaphore_signal(
            barrier, inc=1, device_id={"seq": partner, "head": peers[d]}, device_id_type=pl.DeviceIdType.MESH
        )
    for to in (sibling, up, down):
        pl.semaphore_signal(barrier, inc=1, device_id={"seq": to}, device_id_type=pl.DeviceIdType.MESH)
    kv_piece(0, 0, 0).start()
    kv_piece(0, 0, 1).start()
    q_piece(0, 0).start()
    q_piece(0, 1).start()
    pl.semaphore_wait(barrier, 10)

    for kind in range(2):
        for d in range(1, 4):
            kv_piece(0, d, kind).start()
    for kind in range(2):
        for d in range(4):
            kv_piece(1, d, kind).start()
    for part in range(2):
        for d in range(1, 4):
            q_piece(d, part).start()

    def gathered(xo):
        for kind in range(2):
            for d in range(4):
                if xo == 0 and d == 0:
                    kv_piece(xo, d, kind).wait()
                else:
                    kv_piece(xo, d, kind).wait_recv()
            block = own if xo == 0 else partner // 2
            for way in range(2):
                ring(block, way, 1 + xo, kind).start()
            share(xo, block, kind).start()

    def arrived(pos):
        block, pair, way = block_at(pos), pos // 2, pos % 2

        @pl.when(pair <= 6)
        def _():
            for kind in range(2):
                ring(block, way, pair, kind).wait_recv()
                share(pos, block, kind).start()

                @pl.when(pair <= 4)
                def _():
                    ring(block, way, pair + 2, kind).start()

                @pl.when(jnp.logical_and(pair > 4, way == kind))
                def _():
                    ring(block, way, pair + 2, kind).start()

        @pl.when(pair == 7)
        def _():
            for kind in range(2):
                ring(block, kind, 7 + way, kind).wait_recv()
                share(pos, block, kind).start()

    def shared(pos, block):
        for kind in range(2):
            share(pos, block, kind).wait_recv()

    def heads(u):
        return jnp.concatenate(
            [qb[:, (u * UNIT + i) * HEAD_SIZE : (u * UNIT + i + 1) * HEAD_SIZE] for i in range(UNIT)], axis=0
        )

    def score(u, block, slot, first):
        rows = slice(u * M, (u + 1) * M)
        s = lax.dot_general(heads(u), kv[block, 0], NT, preferred_element_type=F32) * SCALE
        if first:
            token = lax.broadcasted_iota(jnp.int32, (M, BLK), 0) % ROWS + core * ROWS
            s = jnp.where(lax.broadcasted_iota(jnp.int32, (M, BLK), 1) <= token, s, NEG)
        s_s[slot] = s
        top = jnp.broadcast_to(jnp.max(s, axis=1, keepdims=True), (M, HEAD_SIZE))
        if first:
            m_s[rows] = top
            sh_s[slot] = top
        else:
            bias = bias_of(block)
            before = m_s[rows]
            after = jnp.maximum(before, top + bias)
            m_s[rows] = after
            sh_s[slot] = after - bias
            al_s[slot] = jnp.exp2(before - after)

    def weigh(u, block, slot, first):
        rows = slice(u * M, (u + 1) * M)
        shift = sh_s[slot]
        w = jnp.concatenate(
            [
                jnp.exp2(s_s[slot, :, t * HEAD_SIZE : (t + 1) * HEAD_SIZE] - shift).astype(BF16)
                for t in range(BLK // HEAD_SIZE)
            ],
            axis=1,
        )
        ones = jnp.ones((BLK, HEAD_SIZE), BF16)
        part = jnp.dot(w, jnp.concatenate([kv[block, 1], ones], axis=1), preferred_element_type=F32)
        for t in range(2):
            cols = slice(t * HEAD_SIZE, (t + 1) * HEAD_SIZE)
            acc_s[rows, cols] = part[:, cols] if first else acc_s[rows, cols] * al_s[slot] + part[:, cols]

    def finish(u):
        for i in range(UNIT):
            g = u * UNIT + i
            a = acc_s[g * ROWS : (g + 1) * ROWS, :]
            ost[:, g * HEAD_SIZE : (g + 1) * HEAD_SIZE] = (a[:, :HEAD_SIZE] / a[:, HEAD_SIZE:]).astype(BF16)

    gathered(0)
    q_piece(0, 0).wait()
    for d in range(1, 4):
        q_piece(d, 0).wait_recv()
    shared(0, own)
    other = partner // 2
    score(0, own, 0, True)
    score(1, own, 1, True)
    weigh(0, own, 0, True)
    gathered(1)
    q_piece(0, 1).wait()
    for d in range(1, 4):
        q_piece(d, 1).wait_recv()
    score(2, own, 0, True)
    weigh(1, own, 1, True)
    score(3, own, 1, True)
    weigh(2, own, 0, True)
    arrived(2)
    shared(1, other)
    score(0, other, 0, False)
    weigh(3, own, 1, True)

    def one(pos, carry):
        block, after = block_at(pos), block_at(pos + 1)
        for u in range(UNITS - 1):
            score(u + 1, block, (u + 1) % 2, False)
            weigh(u, block, u % 2, False)
            if u == 1:

                @pl.when(pos <= 13)
                def _():
                    arrived(pos + 2)

        shared(pos + 1, after)
        score(0, after, 0, False)
        weigh(UNITS - 1, block, (UNITS - 1) % 2, False)
        return carry

    lax.fori_loop(1, BLOCKS - 1, one, 0)
    last = block_at(BLOCKS - 1)
    for u in range(UNITS):
        if u < UNITS - 1:
            score(u + 1, last, (u + 1) % 2, False)
        weigh(u, last, u % 2, False)
        finish(u)
        for d in range(4):
            out_piece(u, d).start()

    for u in range(UNITS):
        out_piece(u, 0).wait()
        for d in range(1, 4):
            out_piece(u, d).wait()
    for kind in range(2):
        for d in range(1, 4):
            kv_piece(0, d, kind).wait_send()
        for d in range(4):
            kv_piece(1, d, kind).wait_send()
        for step in range(1, 7):
            for way in range(2):
                ring(own, way, step, kind).wait_send()
        for step in range(7, 9):
            ring(own, kind, step, kind).wait_send()
        for pos in range(BLOCKS):
            share(pos, own, kind).wait_send()
    for part in range(2):
        for d in range(1, 4):
            q_piece(d, part).wait_send()


def local(queries, keys, values, page_of_block, links):
    return pl.pallas_call(
        kernel,
        out_shape=jax.ShapeDtypeStruct((TOKENS, 4 * WIDE), BF16),
        in_specs=[pl.BlockSpec(memory_space=pltpu.SMEM)] * 2 + [pl.BlockSpec(memory_space=pl.ANY)] * 3,
        out_specs=pl.BlockSpec(memory_space=pl.ANY),
        scratch_shapes=[
            pltpu.VMEM((BLOCKS, 2, BLK, HEAD_SIZE), BF16),
            pltpu.VMEM((ROWS, WIDE), BF16),
            pltpu.VMEM((ROWS, WIDE), BF16),
            pltpu.VMEM((HEADS * ROWS, HEAD_SIZE), F32),
            pltpu.VMEM((HEADS * ROWS, 2 * HEAD_SIZE), F32),
            pltpu.VMEM((2, M, BLK), F32),
            pltpu.VMEM((2, M, HEAD_SIZE), F32),
            pltpu.VMEM((2, M, HEAD_SIZE), F32),
            pltpu.SemaphoreType.DMA((2, 4, 2)),
            pltpu.SemaphoreType.DMA((2, 4, 2)),
            pltpu.SemaphoreType.DMA((4, 2)),
            pltpu.SemaphoreType.DMA((4, 2)),
            pltpu.SemaphoreType.DMA((2, 9, 2)),
            pltpu.SemaphoreType.DMA((2, 9, 2)),
            pltpu.SemaphoreType.DMA((BLOCKS, 2)),
            pltpu.SemaphoreType.DMA((BLOCKS, 2)),
            pltpu.SemaphoreType.DMA((UNITS, 4)),
            pltpu.SemaphoreType.DMA((UNITS, 4)),
            pltpu.SemaphoreType.DMA((4 + UNITS,)),
        ],
        compiler_params=pltpu.CompilerParams(
            collective_id=0, has_side_effects=True, vmem_limit_bytes=60 * 2**20
        ),
    )(page_of_block, links, queries, keys, values)


def solution(mesh):
    tokens = P(("batch", "seq", "head"), None)
    in_specs = (tokens, tokens, tokens, P("batch"), P("batch", None))
    return jax.shard_map(local, mesh=mesh, in_specs=in_specs, out_specs=tokens, check_vma=False)
```

time: 236 us -> 62.6 us (0.27)
  the two profiles are of different devices: /device:TPU:96 before, /device:TPU:1 now
where the time goes in v1:
time: 62.6 us; the launch traced here: 62.4 us
  Pallas kernels  60.5 us (97%)
  local copies, waits for them, and re-layouts  1.87 us (3%)
    pallas_call x1, Pallas kernels, local(): pl.pallas_call(kernel, out_shape=jax.ShapeDtypeStruct((TOKENS, 4 * WIDE),...  60.5 us
    unnamed x1, local copies, waits for them, and re-layouts  1.87 us

profile of v1, /device:TPU:1, one launch (start us, length us, event | category | flops | bytes accessed | tf_op | source)
XLA Modules:
  0.0 62.4 jit_solution(13148253786520428277)
XLA Ops:
  0.0 60.5 %shard_map.55 = bf16[64,4096]{1,0:T(8,128)(2,1)} custom-call(s32[16]{0:T(128)} %page_ref.1, s32[16,16]{1,0:T(8,128)} %link_ref.1, bf16[64,4096]{1,0:T(8,128)(2,1)} %q_ref.1, bf16[64,512]{1,0:T(8,128)(2,1)} %k_ref.1, bf16[64,512]{1,0:T(8,128)(2,1)} %v_ref.1), custom_call_target="tpu_custom_call" | custom-call | tf_op jit(solution)/shard_map/pallas_call | solution.py:269
  60.6 1.9 %copy.7 = bf16[64,4096]{1,0:T(8,128)(2,1)} copy(bf16[64,4096]{1,0:T(8,128)(2,1)} %shard_map.55) | data formatting | bytes 1048576

commit v2 on v1

--- a/solution.py
+++ b/solution.py
@@ -20,12 +20,13 @@
 NEG = -1e30
 NT = (((1,), (1,)), ((), ()))
 F32, BF16 = jnp.float32, jnp.bfloat16
+EVENT_LEAD, TAIL = 2, 12
 
 
 def kernel(
     page_ref, link_ref, q_ref, k_ref, v_ref, out_ref,
-    kv, qb, ost, m_s, acc_s, s_s, sh_s, al_s,
-    a2a_send, a2a_recv, q_send, q_recv, ring_send, ring_recv, sib_send, sib_recv, out_send, out_recv, loc,
+    kv, qb, ost, m_s, acc_s, s_s, sh_s, al_s, k_st, v_st, q_st,
+    a2a_send, a2a_recv, q_send, q_recv, ring_send, ring_recv, sib_send, sib_recv, out_send, out_recv, loc, stage,
 ):
     seq, head = lax.axis_index("seq"), lax.axis_index("head")
     z, xh, core = seq // 4, (seq // 2) % 2, seq % 2
@@ -43,7 +44,8 @@
         )
 
     def kv_piece(xo, d, kind):
-        src = (k_ref, v_ref)[kind].at[:, pl.ds(pl.multiple_of(peers[d] * HEAD_SIZE, HEAD_SIZE), HEAD_SIZE)]
+        whole = (k_ref, v_ref) if xo == 0 and d == 0 else (k_st, v_st)
+        src = whole[kind].at[:, pl.ds(pl.multiple_of(peers[d] * HEAD_SIZE, HEAD_SIZE), HEAD_SIZE)]
         dst = kv.at[own, kind, pl.ds(pl.multiple_of(core * ROWS + head * TOKENS, TOKENS), TOKENS), :]
         if xo == 0 and d == 0:
             return pltpu.make_async_copy(src, dst, loc.at[kind])
@@ -51,8 +53,10 @@
         return remote(src, dst, a2a_send.at[xo, d, kind], a2a_recv.at[xo, d, kind], **where)
 
     def q_piece(d, part):
-        src = q_ref.at[:, pl.ds(pl.multiple_of(peers[d] * WIDE + part * (WIDE // 2), WIDE // 2), WIDE // 2)]
-        dst = qb.at[pl.ds(pl.multiple_of(head * TOKENS, TOKENS), TOKENS), pl.ds(part * (WIDE // 2), WIDE // 2)]
+        cols = UNIT * HEAD_SIZE
+        whole = q_ref if d == 0 else q_st
+        src = whole.at[:, pl.ds(pl.multiple_of(peers[d] * WIDE + part * cols, cols), cols)]
+        dst = qb.at[pl.ds(pl.multiple_of(head * TOKENS, TOKENS), TOKENS), pl.ds(part * cols, cols)]
         if d == 0:
             return pltpu.make_async_copy(src, dst, loc.at[2 + part])
         return remote(src, dst, q_send.at[d, part], q_recv.at[d, part], head=peers[d])
@@ -68,10 +72,10 @@
 
     def out_piece(u, d):
         cols = UNIT * HEAD_SIZE
-        src = ost.at[pl.ds(pl.multiple_of(peers[d] * TOKENS, TOKENS), TOKENS), pl.ds(u * cols, cols)]
+        src = ost.at[pl.ds(pl.multiple_of(peers[d] * TOKENS, TOKENS), TOKENS), pl.ds(pl.multiple_of(u * cols, cols), cols)]
         dst = out_ref.at[:, pl.ds(pl.multiple_of(head * WIDE + u * cols, cols), cols)]
         if d == 0:
-            return pltpu.make_async_copy(src, dst, loc.at[4 + u])
+            return pltpu.make_async_copy(src, dst, loc.at[2 + UNITS + u])
         return remote(src, dst, out_send.at[u, d], out_recv.at[u, d], head=peers[d])
 
     def block_at(pos):
@@ -95,11 +99,19 @@
         )
     for to in (sibling, up, down):
         pl.semaphore_signal(barrier, inc=1, device_id={"seq": to}, device_id_type=pl.DeviceIdType.MESH)
+    staged = [
+        pltpu.make_async_copy(src, dst, stage.at[i])
+        for i, (src, dst) in enumerate(((k_ref, k_st), (v_ref, v_st), (q_ref, q_st)))
+    ]
+    for copy in staged:
+        copy.start()
     kv_piece(0, 0, 0).start()
     kv_piece(0, 0, 1).start()
-    q_piece(0, 0).start()
-    q_piece(0, 1).start()
+    for part in range(UNITS):
+        q_piece(0, part).start()
     pl.semaphore_wait(barrier, 10)
+    staged[0].wait()
+    staged[1].wait()
 
     for kind in range(2):
         for d in range(1, 4):
@@ -107,7 +119,8 @@
     for kind in range(2):
         for d in range(4):
             kv_piece(1, d, kind).start()
-    for part in range(2):
+    staged[2].wait()
+    for part in range(UNITS):
         for d in range(1, 4):
             q_piece(d, part).start()
 
@@ -123,40 +136,43 @@
                 ring(block, way, 1 + xo, kind).start()
             share(xo, block, kind).start()
 
-    def arrived(pos):
-        block, pair, way = block_at(pos), pos // 2, pos % 2
+    def arrived(event):
+        pair, kind = event // 2 + 1, event % 2
 
         @pl.when(pair <= 6)
         def _():
-            for kind in range(2):
+            for way in range(2):
+                pos = 2 * pair + way
+                block = block_at(pos)
                 ring(block, way, pair, kind).wait_recv()
                 share(pos, block, kind).start()
 
-                @pl.when(pair <= 4)
+                @pl.when(jnp.logical_or(pair <= 4, kind == way))
                 def _():
                     ring(block, way, pair + 2, kind).start()
 
-                @pl.when(jnp.logical_and(pair > 4, way == kind))
-                def _():
-                    ring(block, way, pair + 2, kind).start()
-
         @pl.when(pair == 7)
         def _():
-            for kind in range(2):
-                ring(block, kind, 7 + way, kind).wait_recv()
-                share(pos, block, kind).start()
+            pos = 14 + kind
+            block = block_at(pos)
+            for part in range(2):
+                ring(block, part, 7 + kind, part).wait_recv()
+                share(pos, block, part).start()
 
     def shared(pos, block):
         for kind in range(2):
             share(pos, block, kind).wait_recv()
 
     def heads(u):
-        return jnp.concatenate(
-            [qb[:, (u * UNIT + i) * HEAD_SIZE : (u * UNIT + i + 1) * HEAD_SIZE] for i in range(UNIT)], axis=0
-        )
+        cols = UNIT * HEAD_SIZE
+        q = qb[:, u * cols : (u + 1) * cols] if isinstance(u, int) else qb[:, pl.ds(pl.multiple_of(u * cols, cols), cols)]
+        return jnp.concatenate([q[:, i * HEAD_SIZE : (i + 1) * HEAD_SIZE] for i in range(UNIT)], axis=0)
+
+    def rows_of(u):
+        return slice(u * M, (u + 1) * M) if isinstance(u, int) else pl.ds(pl.multiple_of(u * M, M), M)
 
     def score(u, block, slot, first):
-        rows = slice(u * M, (u + 1) * M)
+        rows = rows_of(u)
         s = lax.dot_general(heads(u), kv[block, 0], NT, preferred_element_type=F32) * SCALE
         if first:
             token = lax.broadcasted_iota(jnp.int32, (M, BLK), 0) % ROWS + core * ROWS
@@ -175,7 +191,7 @@
             al_s[slot] = jnp.exp2(before - after)
 
     def weigh(u, block, slot, first):
-        rows = slice(u * M, (u + 1) * M)
+        rows = rows_of(u)
         shift = sh_s[slot]
         w = jnp.concatenate(
             [
@@ -192,57 +208,79 @@
 
     def finish(u):
         for i in range(UNIT):
-            g = u * UNIT + i
-            a = acc_s[g * ROWS : (g + 1) * ROWS, :]
-            ost[:, g * HEAD_SIZE : (g + 1) * HEAD_SIZE] = (a[:, :HEAD_SIZE] / a[:, HEAD_SIZE:]).astype(BF16)
-
+            a = acc_s[pl.ds(pl.multiple_of((u * UNIT + i) * ROWS, ROWS), ROWS), :]
+            cols = pl.ds(pl.multiple_of((u * UNIT + i) * HEAD_SIZE, HEAD_SIZE), HEAD_SIZE)
+            ost[:, cols] = (a[:, :HEAD_SIZE] / a[:, HEAD_SIZE:]).astype(BF16)
+
+    def queried(part):
+        q_piece(0, part).wait()
+        for d in range(1, 4):
+            q_piece(d, part).wait_recv()
+
+    other = partner // 2
     gathered(0)
-    q_piece(0, 0).wait()
-    for d in range(1, 4):
-        q_piece(d, 0).wait_recv()
+    queried(0)
     shared(0, own)
-    other = partner // 2
     score(0, own, 0, True)
-    score(1, own, 1, True)
     weigh(0, own, 0, True)
     gathered(1)
-    q_piece(0, 1).wait()
-    for d in range(1, 4):
-        q_piece(d, 1).wait_recv()
-    score(2, own, 0, True)
-    weigh(1, own, 1, True)
-    score(3, own, 1, True)
-    weigh(2, own, 0, True)
-    arrived(2)
+    queried(1)
+    score(1, own, 0, True)
+    weigh(1, own, 0, True)
+    arrived(0)
+    queried(2)
     shared(1, other)
     score(0, other, 0, False)
+    score(2, own, 1, True)
+    weigh(0, other, 0, False)
+    score(1, other, 0, False)
+    weigh(2, own, 1, True)
+    weigh(1, other, 0, False)
+    arrived(1)
+    queried(3)
+    score(2, other, 0, False)
+    score(3, own, 1, True)
+    weigh(2, other, 0, False)
+    score(3, other, 0, False)
     weigh(3, own, 1, True)
+    weigh(3, other, 0, False)
+    for event in range(2, 2 + EVENT_LEAD):
+        arrived(event)
+    shared(2, block_at(2))
+    score(0, block_at(2), 0, False)
 
     def one(pos, carry):
         block, after = block_at(pos), block_at(pos + 1)
-        for u in range(UNITS - 1):
-            score(u + 1, block, (u + 1) % 2, False)
+        arrived(pos + EVENT_LEAD)
+        shared(pos + 1, after)
+        for u in range(UNITS):
+            if u < UNITS - 1:
+                score(u + 1, block, (u + 1) % 2, False)
+            else:
+                score(0, after, 0, False)
             weigh(u, block, u % 2, False)
-            if u == 1:
-
-                @pl.when(pos <= 13)
-                def _():
-                    arrived(pos + 2)
-
-        shared(pos + 1, after)
-        score(0, after, 0, False)
-        weigh(UNITS - 1, block, (UNITS - 1) % 2, False)
         return carry
 
-    lax.fori_loop(1, BLOCKS - 1, one, 0)
-    last = block_at(BLOCKS - 1)
-    for u in range(UNITS):
-        if u < UNITS - 1:
-            score(u + 1, last, (u + 1) % 2, False)
-        weigh(u, last, u % 2, False)
+    lax.fori_loop(2, TAIL, one, 0)
+    for event in range(TAIL + EVENT_LEAD, 14):
+        arrived(event)
+    for pos in range(TAIL + 1, BLOCKS):
+        shared(pos, block_at(pos))
+    ends = [block_at(pos) for pos in range(TAIL, BLOCKS)]
+
+    def end(u, carry):
+        for i, block in enumerate(ends):
+            if i < len(ends) - 1:
+                score(u, ends[i + 1], (i + 1) % 2, False)
+            else:
+                score(jnp.minimum(u + 1, UNITS - 1), ends[0], 0, False)
+            weigh(u, block, i % 2, False)
         finish(u)
         for d in range(4):
             out_piece(u, d).start()
+        return carry
+
+    lax.fori_loop(0, UNITS, end, 0)
 
     for u in range(UNITS):
         out_piece(u, 0).wait()
@@ -260,7 +298,7 @@
             ring(own, kind, step, kind).wait_send()
         for pos in range(BLOCKS):
             share(pos, own, kind).wait_send()
-    for part in range(2):
+    for part in range(UNITS):
         for d in range(1, 4):
             q_piece(d, part).wait_send()
 
@@ -280,17 +318,21 @@
             pltpu.VMEM((2, M, BLK), F32),
             pltpu.VMEM((2, M, HEAD_SIZE), F32),
             pltpu.VMEM((2, M, HEAD_SIZE), F32),
+            pltpu.VMEM((TOKENS, 4 * HEAD_SIZE), BF16),
+            pltpu.VMEM((TOKENS, 4 * HEAD_SIZE), BF16),
+            pltpu.VMEM((TOKENS, 4 * WIDE), BF16),
             pltpu.SemaphoreType.DMA((2, 4, 2)),
             pltpu.SemaphoreType.DMA((2, 4, 2)),
-            pltpu.SemaphoreType.DMA((4, 2)),
-            pltpu.SemaphoreType.DMA((4, 2)),
+            pltpu.SemaphoreType.DMA((4, UNITS)),
+            pltpu.SemaphoreType.DMA((4, UNITS)),
             pltpu.SemaphoreType.DMA((2, 9, 2)),
             pltpu.SemaphoreType.DMA((2, 9, 2)),
             pltpu.SemaphoreType.DMA((BLOCKS, 2)),
             pltpu.SemaphoreType.DMA((BLOCKS, 2)),
             pltpu.SemaphoreType.DMA((UNITS, 4)),
             pltpu.SemaphoreType.DMA((UNITS, 4)),
-            pltpu.SemaphoreType.DMA((4 + UNITS,)),
+            pltpu.SemaphoreType.DMA((2 + 2 * UNITS,)),
+            pltpu.SemaphoreType.DMA((3,)),
         ],
         compiler_params=pltpu.CompilerParams(
             collective_id=0, has_side_effects=True, vmem_limit_bytes=60 * 2**20

time: 62.6 us -> 55.6 us (0.89)
  Pallas kernels: 60.5 us -> 53.5 us
    pallas_call x1, Pallas kernels: 60.5 us -> 53.5 us  [local(): pl.pallas_call(kernel, out_shape=jax.ShapeDtypeStruct((TOKENS, 4 * WIDE),...]
where the time goes in v2:
time: 55.6 us; the launch traced here: 55.4 us
  Pallas kernels  53.5 us (96%)
  local copies, waits for them, and re-layouts  1.87 us (3%)
    pallas_call x1, Pallas kernels, local(): pl.pallas_call(kernel, out_shape=jax.ShapeDtypeStruct((TOKENS, 4 * WIDE),...  53.5 us
    unnamed x1, local copies, waits for them, and re-layouts  1.87 us

profile of v2, /device:TPU:1, one launch (start us, length us, event | category | flops | bytes accessed | tf_op | source)
XLA Modules:
  0.0 55.4 jit_solution(15605249769719447627)
XLA Ops:
  0.0 53.5 %shard_map.55 = bf16[64,4096]{1,0:T(8,128)(2,1)} custom-call(s32[16]{0:T(128)} %page_ref.1, s32[16,16]{1,0:T(8,128)} %link_ref.1, bf16[64,4096]{1,0:T(8,128)(2,1)} %q_ref.1, bf16[64,512]{1,0:T(8,128)(2,1)} %k_ref.1, bf16[64,512]{1,0:T(8,128)(2,1)} %v_ref.1), custom_call_target="tpu_custom_call" | custom-call | tf_op jit(solution)/shard_map/pallas_call | solution.py:307
  53.5 1.9 %copy.7 = bf16[64,4096]{1,0:T(8,128)(2,1)} copy(bf16[64,4096]{1,0:T(8,128)(2,1)} %shard_map.55) | data formatting | bytes 1048576
